TPU v7x, 32 devices: a whole 2x2x4 slice. The times are simulated.
32 devices in a mesh: half: 2 (over core), grp: 16 (over z, y, x).
Axes of the slice: x: 2, y: 2, z: 4, core: 2. Of those that a mesh axis runs over, the one named last changes fastest.
Arguments:
- weights: float32 [2, 16, 2, 8192, 128], P('half', 'grp'), may hold values from -4 to 4
- accum: float32 [2, 16, 2, 8192], P('half', 'grp'), may hold values from 0.01 to 1
- grads: float32 [32, 32, 16, 128], P(('half', 'grp')), may hold values from -6 to 6
- row_ids: int32 [32, 32, 16], P(('half', 'grp')), may hold values from 0 to 16383
- counts: int32 [32, 32], P(('half', 'grp')), may hold values from 1 to 16, as said below
Outputs:
- new_weights: float32 [2, 16, 2, 8192, 128], P('half', 'grp')
- new_accum: float32 [2, 16, 2, 8192], P('half', 'grp')
Inputs may be any that keep to these rules, and one draw needn't show every extreme that they name: `counts`: A few owners, the same for all senders, receive 16 live rows from every sender; no two of them share a shard index g (owners g and 16 + g). The owner that shares its shard index with such an owner receives 16 // 2 live rows from every sender; each other count lies from 1 to 8. So the two owners of one shard index receive at most 24 live rows from one sender together, and some pair receives exactly that.
All inputs are finite; a program needn't handle non-finite values.
Results may differ from a plain program's by a relative error of at most 0.00002.
Values sent between devices are 32-bit elements; how exact they have to be, the bound alone decides.
A program may use at most 128 MiB of HBM per device.

v0:
```python
import functools

import jax
import jax.numpy as jnp
from jax import lax
from jax.experimental import pallas as pl
from jax.experimental.pallas import tpu as pltpu
from jax.sharding import PartitionSpec as P

LEARN_RATE = 0.5
EPSILON = 1e-06
LANES = 128
MESH = pl.DeviceIdType.MESH
PIECES = 4


def exchange_kernel(
    halves, groups, weights, accum, grads, ids_t, counts,
    table, pair_acc, got, got_ids,
    block_buf, id_in, count_in, id_pad, id_buf,
    local_sem, row_send, row_recv, acc_send, acc_recv, block_send, block_recv, id_send, id_recv,
):
    half = lax.axis_index("half")
    group = lax.axis_index("grp")
    owners = halves * groups
    me = half * groups + group
    other = 1 - half
    slots = ids_t.shape[0]
    rows_half = weights.shape[1]
    piece = rows_half // PIECES
    home = pl.multiple_of(half * rows_half, rows_half)

    def peer_of(step):
        peer = lax.rem(me + step, owners)
        return peer, (peer // groups, lax.rem(peer, groups))

    barrier = pltpu.get_barrier_semaphore()

    @pl.loop(1, owners)
    def _(step):
        _, where = peer_of(step)
        pl.semaphore_signal(barrier, inc=1, device_id=where, device_id_type=MESH)

    id_load = pltpu.make_async_copy(ids_t, id_in, local_sem.at[1])
    count_load = pltpu.make_async_copy(counts, count_in, local_sem.at[2])
    load = pltpu.make_async_copy(grads, block_buf, local_sem.at[0])
    keep = pltpu.make_async_copy(
        weights.at[half], table.at[pl.ds(home, rows_half)], local_sem.at[3])
    keep_acc = pltpu.make_async_copy(accum, pair_acc.at[half], local_sem.at[4])
    id_load.start()
    count_load.start()
    keep_acc.start()
    load.start()
    keep.start()
    id_load.wait()
    count_load.wait()
    slot = lax.broadcasted_iota(jnp.int32, ids_t.shape, 0)
    id_pad[...] = jnp.full(id_pad.shape, -1, jnp.int32)
    id_pad[0:slots, 0:owners] = jnp.where(slot < count_in[...], id_in[...], -1)
    turned = id_pad[...].T
    for owner in range(owners):
        id_buf[owner, 0:1, :] = turned[owner:owner + 1, :]
    load.wait()
    pl.semaphore_wait(barrier, owners - 1)

    def block_copy(step):
        peer, where = peer_of(step)
        return pltpu.make_async_remote_copy(
            src_ref=block_buf.at[peer], dst_ref=got.at[me],
            send_sem=block_send.at[peer], recv_sem=block_recv.at[me],
            device_id=where, device_id_type=MESH)

    def id_copy(step):
        peer, where = peer_of(step)
        return pltpu.make_async_remote_copy(
            src_ref=id_buf.at[peer], dst_ref=got_ids.at[me],
            send_sem=id_send.at[peer], recv_sem=id_recv.at[me],
            device_id=where, device_id_type=MESH)

    def row_copy(index):
        rows = pl.ds(index * piece, piece)
        return pltpu.make_async_remote_copy(
            src_ref=weights.at[other, rows],
            dst_ref=table.at[pl.ds(pl.multiple_of(home + index * piece, piece), piece)],
            send_sem=row_send.at[index], recv_sem=row_recv.at[index],
            device_id=(other, group), device_id_type=MESH)

    acc_copy = pltpu.make_async_remote_copy(
        src_ref=accum, dst_ref=pair_acc.at[half], send_sem=acc_send, recv_sem=acc_recv,
        device_id=(other, group), device_id_type=MESH)

    @pl.loop(1, owners)
    def _(step):
        id_copy(step).start()
        block_copy(step).start()

    acc_copy.start()
    for index in range(PIECES):
        row_copy(index).start()
    own_block = pltpu.make_async_copy(block_buf.at[me], got.at[me], local_sem.at[0])
    own_ids = pltpu.make_async_copy(id_buf.at[me], got_ids.at[me], local_sem.at[1])
    own_block.start()
    own_ids.start()
    own_block.wait()
    own_ids.wait()
    keep.wait()
    keep_acc.wait()

    @pl.loop(1, owners)
    def _(step):
        id_copy(step).wait_send()
        block_copy(step).wait_send()
        peer, where = peer_of(step)
        pltpu.make_async_remote_copy(
            src_ref=id_buf.at[peer], dst_ref=got_ids.at[peer],
            send_sem=id_send.at[peer], recv_sem=id_recv.at[peer],
            device_id=where, device_id_type=MESH).wait_recv()
        pltpu.make_async_remote_copy(
            src_ref=block_buf.at[peer], dst_ref=got.at[peer],
            send_sem=block_send.at[peer], recv_sem=block_recv.at[peer],
            device_id=where, device_id_type=MESH).wait_recv()

    acc_copy.wait()
    for index in range(PIECES):
        row_copy(index).wait()


def thirds(value):
    first = value.astype(jnp.bfloat16)
    rest = value - first.astype(jnp.float32)
    second = rest.astype(jnp.bfloat16)
    third = (rest - second.astype(jnp.float32)).astype(jnp.bfloat16)
    return jnp.concatenate([first, second, third], axis=1)


def joined(value, width):
    return value[:, 0:width] + value[:, width:2 * width] + value[:, 2 * width:3 * width]


def update_kernel(
    table_in, pair_acc, got, got_ids, table, new_weights, new_accum,
    out_acc, state, id_list, picked, delta, in_sem, out_sem, id_sem,
):
    half = lax.axis_index("half")
    senders, slots, width = got.shape
    count = senders * slots
    rows_half = pair_acc.shape[2]
    piece = rows_half // PIECES
    spare = 2 * rows_half
    acc_rows = rows_half // LANES

    ids_in = pltpu.make_async_copy(got_ids, id_list, id_sem)
    ids_in.start()
    table[spare:spare + 8, :] = jnp.zeros((8, width), jnp.float32)

    is_low = half == 0
    for old in range(2):
        line = jnp.where(is_low, pair_acc[old, 0:1, :], pair_acc[old, 1:2, :])
        for row in range(acc_rows):
            at = old * acc_rows + row
            state[at:at + 1, :] = line[:, row * LANES:(row + 1) * LANES]

    lane = lax.broadcasted_iota(jnp.int32, (count, LANES), 1)
    sub = lax.broadcasted_iota(jnp.int32, (count, LANES), 0)
    spread = jnp.broadcast_to(got_ids[...], (senders, slots, LANES)).reshape(count, LANES)
    mine = jnp.where(lane == lax.rem(sub, slots), spread, 0).astype(jnp.float32)
    column = jnp.sum(mine, axis=1, keepdims=True)
    wide = jnp.broadcast_to(column, (count, LANES))
    line = wide.T[0:1, :]
    grad_parts = thirds(got[...].reshape(count, width))
    old_state = state[...]
    state_parts = thirds(old_state)
    lane_f = lane.astype(jnp.float32)
    block = min(count, 512)
    gain = jnp.zeros((2 * acc_rows, 3 * LANES), jnp.float32)
    high_line = jnp.floor(line * (1.0 / LANES))
    for start in range(0, count, block):
        key = column[start:start + block]
        same = key == line
        hot = jnp.where(same, 1.0, 0.0)
        total = joined(jnp.dot(hot.astype(jnp.bfloat16), grad_parts,
                               preferred_element_type=jnp.float32), width)
        at_col = lax.broadcasted_iota(jnp.int32, (block, count), 1)
        at_row = lax.broadcasted_iota(jnp.int32, (block, count), 0) + start
        earlier = jnp.sum(jnp.where(at_col < at_row, hot, 0.0), axis=1, keepdims=True)
        high = jnp.floor(key * (1.0 / LANES))
        low = key - high * LANES
        row_hot = jnp.where(lane_f[:block] == high, 1.0, 0.0).astype(jnp.bfloat16) if acc_rows * 2 == LANES else jnp.where(
            lax.broadcasted_iota(jnp.int32, (block, 2 * acc_rows), 1).astype(jnp.float32) == high, 1.0, 0.0).astype(jnp.bfloat16)
        state_rows = joined(jnp.dot(row_hot, state_parts, preferred_element_type=jnp.float32), LANES)
        at_low = lane_f[:block] == low
        old_acc = jnp.sum(jnp.where(at_low, state_rows, 0.0), axis=1, keepdims=True)
        square = jnp.sum(total * total, axis=1, keepdims=True) * (1.0 / width)
        delta[start:start + block, :] = LEARN_RATE * total / (jnp.sqrt(old_acc + square) + EPSILON)
        once = jnp.where((earlier == 0.0) & (key >= 0.0), square, 0.0)
        add_parts = thirds(jnp.where(at_low, once, 0.0))
        high_of = high_line[:, start:start + block]
        tall = lax.broadcasted_iota(jnp.int32, (2 * acc_rows, block), 0).astype(jnp.float32)
        tall_hot = jnp.where(tall == high_of, 1.0, 0.0).astype(jnp.bfloat16)
        gain = gain + jnp.dot(tall_hot, add_parts, preferred_element_type=jnp.float32)
    state[...] = old_state + joined(gain, LANES)
    for old in range(2):
        for row in range(acc_rows):
            at = old * acc_rows + row
            out_acc[old:old + 1, row * LANES:(row + 1) * LANES] = state[at:at + 1, :]

    acc_out = pltpu.make_async_copy(out_acc, new_accum, in_sem)
    acc_out.start()
    ids_in.wait()

    def place(sender, slot):
        at = id_list[sender, 0, slot]
        return jnp.where(at < 0, spare, at)

    @pl.loop(0, senders)
    def _(sender):
        base = pl.multiple_of(sender * slots, slots)
        rows = [table[pl.ds(place(sender, slot), 1), :] for slot in range(slots)]
        for slot in range(slots):
            picked[pl.ds(base + slot, 1), :] = rows[slot]

    picked[...] = picked[...] - delta[...]

    @pl.loop(0, senders)
    def _(sender):
        base = pl.multiple_of(sender * slots, slots)
        rows = [picked[pl.ds(base + slot, 1), :] for slot in range(slots)]
        for slot in range(slots):
            table[pl.ds(place(sender, slot), 1), :] = rows[slot]

    stores = []
    for old in range(2):
        for index in range(PIECES):
            stores.append(pltpu.make_async_copy(
                table.at[pl.ds(old * rows_half + index * piece, piece)],
                new_weights.at[old, pl.ds(index * piece, piece)],
                out_sem.at[old * PIECES + index]))
    for store in stores:
        store.start()
    for store in stores:
        store.wait()
    acc_out.wait()


def per_device(halves, groups, weights, accum, grads, row_ids, counts):
    owners, slots, width = grads.shape[1:]
    rows_half = weights.shape[3]
    table = weights[0, 0]
    state = accum[0, 0]
    count = owners * slots
    hbm = pl.BlockSpec(memory_space=pltpu.HBM)
    vmem = pl.BlockSpec(memory_space=pltpu.VMEM)
    id_width = -(-owners // LANES) * LANES
    dma = pltpu.SemaphoreType.DMA
    landed = (
        jax.ShapeDtypeStruct((2 * rows_half + 8, width), jnp.float32),
        jax.ShapeDtypeStruct((2, 2, rows_half), jnp.float32),
        jax.ShapeDtypeStruct((owners, slots, width), jnp.float32),
        jax.ShapeDtypeStruct((owners, 1, LANES), jnp.int32),
    )
    moved, pair_acc, got, got_ids = pl.pallas_call(
        functools.partial(exchange_kernel, halves, groups),
        out_shape=landed,
        in_specs=[hbm] * 5,
        out_specs=(vmem,) * 4,
        scratch_shapes=[
            pltpu.VMEM((owners, slots, width), jnp.float32),
            pltpu.VMEM((slots, owners), jnp.int32),
            pltpu.VMEM((1, owners), jnp.int32),
            pltpu.VMEM((LANES, id_width), jnp.int32),
            pltpu.VMEM((owners, 1, LANES), jnp.int32),
            dma((5,)),
            dma((PIECES,)), dma((PIECES,)),
            dma, dma,
            dma((owners,)), dma((owners,)),
            dma((owners,)), dma((owners,)),
        ],
        compiler_params=pltpu.CompilerParams(
            collective_id=0, has_side_effects=True, vmem_limit_bytes=16 << 20),
        name="exchange",
    )(*(pltpu.with_memory_space_constraint(value, pltpu.HBM)
        for value in (table, state, grads[0], row_ids[0].T, counts)))
    _, new_weights, new_accum = pl.pallas_call(
        update_kernel,
        out_shape=(
            jax.ShapeDtypeStruct((2 * rows_half + 8, width), jnp.float32),
            jax.ShapeDtypeStruct((2, rows_half, width), jnp.float32),
            jax.ShapeDtypeStruct((2, rows_half), jnp.float32),
        ),
        in_specs=[vmem] * 4,
        out_specs=(vmem, hbm, hbm),
        scratch_shapes=[
            pltpu.VMEM((2, rows_half), jnp.float32),
            pltpu.VMEM((2 * rows_half // LANES, LANES), jnp.float32),
            pltpu.SMEM((owners, 1, LANES), jnp.int32),
            pltpu.VMEM((count, width), jnp.float32),
            pltpu.VMEM((count, width), jnp.float32),
            dma, dma((2 * PIECES,)), dma,
        ],
        input_output_aliases={0: 0},
        compiler_params=pltpu.CompilerParams(vmem_limit_bytes=32 << 20),
        name="update",
    )(moved, pair_acc, got, got_ids)
    return new_weights[None, None], new_accum[None, None]


def solution(mesh):
    placed = (
        P("half", "grp", None, None, None),
        P("half", "grp", None, None),
        P(("half", "grp"), None, None, None),
        P(("half", "grp"), None, None),
        P(("half", "grp"), None),
    )
    return jax.shard_map(
        functools.partial(per_device, mesh.shape["half"], mesh.shape["grp"]),
        mesh=mesh,
        in_specs=placed,
        out_specs=(P("half", "grp", None, None, None), P("half", "grp", None, None)),
        check_vma=False,
    )
```

profile of v0, /device:TPU:0, one launch (start us, length us, event | category | flops | bytes accessed | tf_op | source)
XLA Modules:
  0.0 23.1 jit_solution(3516684785238067607)
XLA Ops:
  0.6 16.3 %exchange.1 = (f32[16392,128]{1,0:T(8,128)S(1)}, f32[2,2,8192]{2,1,0:T(2,128)S(1)}, f32[32,16,128]{2,1,0:T(8,128)S(1)}, s32[32,1,128]{2,1,0:T(1,128)S(1)}) custom-call(f32[2,8192,128]{2,1,0:T(8,128)} %bitcast.8, f32[2,8192]{1,0:T(2,128)} %bitcast.10, f32[32,16,128]{2,1,0:T(8,128)} %bitcast.9, s32[16,32]{1,0:T(8,128)} %bitcast.11, s32[1,32]{1,0:T(1,128)} %counts.1), custom_call_target="tpu_custom_call" | custom-call | tf_op jit(solution)/shard_map/exchange/pallas_call | solution.py:261
  17.0 6.1 %update.1 = (f32[16392,128]{1,0:T(8,128)S(1)}, f32[2,8192,128]{2,1,0:T(8,128)}, f32[2,8192]{1,0:T(2,128)}) custom-call(f32[16392,128]{1,0:T(8,128)S(1)} %get-tuple-element.8.table_in, f32[2,2,8192]{2,1,0:T(2,128)S(1)} %get-tuple-element.9.pair_acc, f32[32,16,128]{2,1,0:T(8,128)S(1)} %get-tuple-element.10.got, ...), custom_call_target="tpu_custom_call", output_to_operand_aliasing={{0}: (0, {})} | custom-call | tf_op jit(solution)/shard_map/update/pallas_call | solution.py:283
where the time goes:
time: 23.3 us; the launch traced here: 23.1 us
  Pallas kernels  22.5 us (97%)
  between operations  0.64 us (3%)
    pallas_call x1, Pallas kernels, per_device(): pl.pallas_call(functools.partial(exchange_kernel, halves, groups), out_sh...  16.3 us
    pallas_call x1, Pallas kernels, per_device(): pl.pallas_call(update_kernel, out_shape=(jax.ShapeDtypeStruct((2 * rows_h...  6.15 us

commit v1 on v0

--- a/solution.py
+++ b/solution.py
@@ -18,7 +18,7 @@
     halves, groups, weights, accum, grads, ids_t, counts,
     table, pair_acc, got, got_ids,
     block_buf, id_in, count_in, id_pad, id_buf,
-    local_sem, row_send, row_recv, acc_send, acc_recv, block_send, block_recv, id_send, id_recv,
+    local_sem, row_send, row_recv, acc_send, acc_recv, block_send, block_recv, id_send, id_recv, ready,
 ):
     half = lax.axis_index("half")
     group = lax.axis_index("grp")
@@ -30,17 +30,8 @@
     piece = rows_half // PIECES
     home = pl.multiple_of(half * rows_half, rows_half)
 
-    def peer_of(step):
-        peer = lax.rem(me + step, owners)
-        return peer, (peer // groups, lax.rem(peer, groups))
-
     barrier = pltpu.get_barrier_semaphore()
-
-    @pl.loop(1, owners)
-    def _(step):
-        _, where = peer_of(step)
-        pl.semaphore_signal(barrier, inc=1, device_id=where, device_id_type=MESH)
-
+    pl.semaphore_signal(barrier, inc=1, device_id=(other, group), device_id_type=MESH)
     id_load = pltpu.make_async_copy(ids_t, id_in, local_sem.at[1])
     count_load = pltpu.make_async_copy(counts, count_in, local_sem.at[2])
     load = pltpu.make_async_copy(grads, block_buf, local_sem.at[0])
@@ -49,9 +40,13 @@
     keep_acc = pltpu.make_async_copy(accum, pair_acc.at[half], local_sem.at[4])
     id_load.start()
     count_load.start()
-    keep_acc.start()
     load.start()
-    keep.start()
+
+    @pl.loop(group + 1, groups)
+    def _(peer_group):
+        for peer_half in range(halves):
+            pl.semaphore_signal(barrier, inc=1, device_id=(peer_half, peer_group), device_id_type=MESH)
+
     id_load.wait()
     count_load.wait()
     slot = lax.broadcasted_iota(jnp.int32, ids_t.shape, 0)
@@ -60,22 +55,29 @@
     turned = id_pad[...].T
     for owner in range(owners):
         id_buf[owner, 0:1, :] = turned[owner:owner + 1, :]
-    load.wait()
-    pl.semaphore_wait(barrier, owners - 1)
-
-    def block_copy(step):
-        peer, where = peer_of(step)
+    pl.semaphore_wait(barrier, halves * group + 1)
+
+    @pl.loop(0, group)
+    def _(peer_group):
+        for peer_half in range(halves):
+            pl.semaphore_signal(
+                ready.at[group], inc=1, device_id=(peer_half, peer_group), device_id_type=MESH)
+
+    def block_copy(peer_half, peer_group, lands=None):
+        peer = peer_half * groups + peer_group
+        at = me if lands is None else peer
         return pltpu.make_async_remote_copy(
-            src_ref=block_buf.at[peer], dst_ref=got.at[me],
-            send_sem=block_send.at[peer], recv_sem=block_recv.at[me],
-            device_id=where, device_id_type=MESH)
-
-    def id_copy(step):
-        peer, where = peer_of(step)
+            src_ref=block_buf.at[peer], dst_ref=got.at[at],
+            send_sem=block_send.at[peer], recv_sem=block_recv.at[at],
+            device_id=(peer_half, peer_group), device_id_type=MESH)
+
+    def id_copy(peer_half, peer_group, lands=None):
+        peer = peer_half * groups + peer_group
+        at = me if lands is None else peer
         return pltpu.make_async_remote_copy(
-            src_ref=id_buf.at[peer], dst_ref=got_ids.at[me],
-            send_sem=id_send.at[peer], recv_sem=id_recv.at[me],
-            device_id=where, device_id_type=MESH)
+            src_ref=id_buf.at[peer], dst_ref=got_ids.at[at],
+            send_sem=id_send.at[peer], recv_sem=id_recv.at[at],
+            device_id=(peer_half, peer_group), device_id_type=MESH)
 
     def row_copy(index):
         rows = pl.ds(index * piece, piece)
@@ -88,41 +90,60 @@
     acc_copy = pltpu.make_async_remote_copy(
         src_ref=accum, dst_ref=pair_acc.at[half], send_sem=acc_send, recv_sem=acc_recv,
         device_id=(other, group), device_id_type=MESH)
-
-    @pl.loop(1, owners)
-    def _(step):
-        id_copy(step).start()
-        block_copy(step).start()
-
     acc_copy.start()
     for index in range(PIECES):
         row_copy(index).start()
+
+    @pl.loop(0, group)
+    def _(peer_group):
+        for peer_half in range(halves):
+            id_copy(peer_half, peer_group).start()
+
+    load.wait()
+
+    @pl.loop(0, group)
+    def _(peer_group):
+        for peer_half in range(halves):
+            block_copy(peer_half, peer_group).start()
+
+    id_copy(other, group).start()
+    block_copy(other, group).start()
+    keep.start()
+    keep_acc.start()
     own_block = pltpu.make_async_copy(block_buf.at[me], got.at[me], local_sem.at[0])
     own_ids = pltpu.make_async_copy(id_buf.at[me], got_ids.at[me], local_sem.at[1])
     own_block.start()
     own_ids.start()
+
+    @pl.loop(group + 1, groups)
+    def _(peer_group):
+        pl.semaphore_wait(ready.at[peer_group], halves)
+        for peer_half in range(halves):
+            id_copy(peer_half, peer_group).start()
+            block_copy(peer_half, peer_group).start()
+
     own_block.wait()
     own_ids.wait()
-    keep.wait()
-    keep_acc.wait()
-
-    @pl.loop(1, owners)
+
+    def finish(peer_half, peer_group):
+        id_copy(peer_half, peer_group).wait_send()
+        block_copy(peer_half, peer_group).wait_send()
+        id_copy(peer_half, peer_group, "here").wait_recv()
+        block_copy(peer_half, peer_group, "here").wait_recv()
+
+    finish(other, group)
+
+    @pl.loop(1, groups)
     def _(step):
-        id_copy(step).wait_send()
-        block_copy(step).wait_send()
-        peer, where = peer_of(step)
-        pltpu.make_async_remote_copy(
-            src_ref=id_buf.at[peer], dst_ref=got_ids.at[peer],
-            send_sem=id_send.at[peer], recv_sem=id_recv.at[peer],
-            device_id=where, device_id_type=MESH).wait_recv()
-        pltpu.make_async_remote_copy(
-            src_ref=block_buf.at[peer], dst_ref=got.at[peer],
-            send_sem=block_send.at[peer], recv_sem=block_recv.at[peer],
-            device_id=where, device_id_type=MESH).wait_recv()
+        peer_group = lax.rem(group + step, groups)
+        for peer_half in range(halves):
+            finish(peer_half, peer_group)
 
     acc_copy.wait()
     for index in range(PIECES):
         row_copy(index).wait()
+    keep.wait()
+    keep_acc.wait()
 
 
 def thirds(value):
@@ -274,6 +295,7 @@
             dma, dma,
             dma((owners,)), dma((owners,)),
             dma((owners,)), dma((owners,)),
+            pltpu.SemaphoreType.REGULAR((groups,)),
         ],
         compiler_params=pltpu.CompilerParams(
             collective_id=0, has_side_effects=True, vmem_limit_bytes=16 << 20),

time: 23.3 us -> 21 us (0.901)
  the two profiles are of different devices: /device:TPU:0 before, /device:TPU:25 now
where the time goes in v1:
time: 21 us; the launch traced here: 20.8 us
  Pallas kernels  20.2 us (96%)
  between operations  0.64 us (3%)
    pallas_call x1, Pallas kernels, per_device(): pl.pallas_call(functools.partial(exchange_kernel, halves, groups), out_sh...  14.1 us
    pallas_call x1, Pallas kernels, per_device(): pl.pallas_call(update_kernel, out_shape=(jax.ShapeDtypeStruct((2 * rows_h...  6.15 us

profile of v1, /device:TPU:25, one launch (start us, length us, event | category | flops | bytes accessed | tf_op | source)
XLA Modules:
  0.0 20.8 jit_solution(11665010494163188501)
XLA Ops:
  0.6 14.1 %exchange.1 = (f32[16392,128]{1,0:T(8,128)S(1)}, f32[2,2,8192]{2,1,0:T(2,128)S(1)}, f32[32,16,128]{2,1,0:T(8,128)S(1)}, s32[32,1,128]{2,1,0:T(1,128)S(1)}) custom-call(f32[2,8192,128]{2,1,0:T(8,128)} %bitcast.8, f32[2,8192]{1,0:T(2,128)} %bitcast.10, f32[32,16,128]{2,1,0:T(8,128)} %bitcast.9, s32[16,32]{1,0:T(8,128)} %bitcast.11, s32[1,32]{1,0:T(1,128)} %counts.1), custom_call_target="tpu_custom_call" | custom-call | tf_op jit(solution)/shard_map/exchange/pallas_call | solution.py:282
  14.7 6.2 %update.1 = (f32[16392,128]{1,0:T(8,128)S(1)}, f32[2,8192,128]{2,1,0:T(8,128)}, f32[2,8192]{1,0:T(2,128)}) custom-call(f32[16392,128]{1,0:T(8,128)S(1)} %get-tuple-element.8.table_in, f32[2,2,8192]{2,1,0:T(2,128)S(1)} %get-tuple-element.9.pair_acc, f32[32,16,128]{2,1,0:T(8,128)S(1)} %get-tuple-element.10.got, ...), custom_call_target="tpu_custom_call", output_to_operand_aliasing={{0}: (0, {})} | custom-call | tf_op jit(solution)/shard_map/update/pallas_call | solution.py:305

commit v2 on v1

--- a/solution.py
+++ b/solution.py
@@ -1,4 +1,5 @@
 import functools
+import math
 
 import jax
 import jax.numpy as jnp
@@ -12,6 +13,13 @@
 LANES = 128
 MESH = pl.DeviceIdType.MESH
 PIECES = 4
+
+
+def axes_of(groups):
+    first = 4 if groups % 4 == 0 else groups
+    rest = groups // first
+    side = math.isqrt(rest)
+    return (first, side, side) if side * side == rest else (first, rest, 1)
 
 
 def exchange_kernel(
@@ -30,6 +38,33 @@
     piece = rows_half // PIECES
     home = pl.multiple_of(half * rows_half, rows_half)
 
+    size_a, size_b, size_c = axes_of(groups)
+    at_a = group // (size_b * size_c)
+    at_b = lax.rem(group // size_c, size_b)
+    at_c = lax.rem(group, size_c)
+
+    def box(low, high, act):
+        @pl.loop(low[0], high[0])
+        def _(a):
+            @pl.loop(low[1], high[1])
+            def _(b):
+                @pl.loop(low[2], high[2])
+                def _(c):
+                    peer_group = (a * size_b + b) * size_c + c
+
+                    @pl.when(peer_group != group)
+                    def _():
+                        act(peer_group, (a, b, c))
+
+    here = (at_a, at_b, at_c)
+    past = (at_a + 1, at_b + 1, at_c + 1)
+
+    def descendants(act):
+        box(here, (size_a, size_b, size_c), act)
+
+    def ancestors(act):
+        box((0, 0, 0), past, act)
+
     barrier = pltpu.get_barrier_semaphore()
     pl.semaphore_signal(barrier, inc=1, device_id=(other, group), device_id_type=MESH)
     id_load = pltpu.make_async_copy(ids_t, id_in, local_sem.at[1])
@@ -42,11 +77,11 @@
     count_load.start()
     load.start()
 
-    @pl.loop(group + 1, groups)
-    def _(peer_group):
+    def greet(peer_group, _):
         for peer_half in range(halves):
             pl.semaphore_signal(barrier, inc=1, device_id=(peer_half, peer_group), device_id_type=MESH)
 
+    descendants(greet)
     id_load.wait()
     count_load.wait()
     slot = lax.broadcasted_iota(jnp.int32, ids_t.shape, 0)
@@ -55,29 +90,35 @@
     turned = id_pad[...].T
     for owner in range(owners):
         id_buf[owner, 0:1, :] = turned[owner:owner + 1, :]
-    pl.semaphore_wait(barrier, halves * group + 1)
-
-    @pl.loop(0, group)
-    def _(peer_group):
+    load.wait()
+    pl.semaphore_wait(barrier, halves * past[0] * past[1] * past[2] - 1)
+
+    def announce(peer_group, _):
         for peer_half in range(halves):
             pl.semaphore_signal(
                 ready.at[group], inc=1, device_id=(peer_half, peer_group), device_id_type=MESH)
 
-    def block_copy(peer_half, peer_group, lands=None):
-        peer = peer_half * groups + peer_group
-        at = me if lands is None else peer
+    ancestors(announce)
+
+    def block_copy(peer_half, peer_group):
         return pltpu.make_async_remote_copy(
-            src_ref=block_buf.at[peer], dst_ref=got.at[at],
-            send_sem=block_send.at[peer], recv_sem=block_recv.at[at],
+            src_ref=block_buf.at[peer_half * groups + peer_group], dst_ref=got.at[me],
+            send_sem=block_send, recv_sem=block_recv,
             device_id=(peer_half, peer_group), device_id_type=MESH)
 
-    def id_copy(peer_half, peer_group, lands=None):
-        peer = peer_half * groups + peer_group
-        at = me if lands is None else peer
+    def id_copy(peer_half, peer_group):
         return pltpu.make_async_remote_copy(
-            src_ref=id_buf.at[peer], dst_ref=got_ids.at[at],
-            send_sem=id_send.at[peer], recv_sem=id_recv.at[at],
+            src_ref=id_buf.at[peer_half * groups + peer_group], dst_ref=got_ids.at[me],
+            send_sem=id_send, recv_sem=id_recv,
             device_id=(peer_half, peer_group), device_id_type=MESH)
+
+    def send_ids(peer_group, _):
+        for peer_half in range(halves):
+            id_copy(peer_half, peer_group).start()
+
+    def send_block(peer_group, _):
+        for peer_half in range(halves):
+            block_copy(peer_half, peer_group).start()
 
     def row_copy(index):
         rows = pl.ds(index * piece, piece)
@@ -93,57 +134,42 @@
     acc_copy.start()
     for index in range(PIECES):
         row_copy(index).start()
-
-    @pl.loop(0, group)
-    def _(peer_group):
-        for peer_half in range(halves):
-            id_copy(peer_half, peer_group).start()
-
-    load.wait()
-
-    @pl.loop(0, group)
-    def _(peer_group):
-        for peer_half in range(halves):
-            block_copy(peer_half, peer_group).start()
-
+    ancestors(send_ids)
+    ancestors(send_block)
     id_copy(other, group).start()
     block_copy(other, group).start()
     keep.start()
     keep_acc.start()
-    own_block = pltpu.make_async_copy(block_buf.at[me], got.at[me], local_sem.at[0])
-    own_ids = pltpu.make_async_copy(id_buf.at[me], got_ids.at[me], local_sem.at[1])
-    own_block.start()
-    own_ids.start()
-
-    @pl.loop(group + 1, groups)
-    def _(peer_group):
-        pl.semaphore_wait(ready.at[peer_group], halves)
-        for peer_half in range(halves):
-            id_copy(peer_half, peer_group).start()
-            block_copy(peer_half, peer_group).start()
-
-    own_block.wait()
-    own_ids.wait()
-
-    def finish(peer_half, peer_group):
-        id_copy(peer_half, peer_group).wait_send()
-        block_copy(peer_half, peer_group).wait_send()
-        id_copy(peer_half, peer_group, "here").wait_recv()
-        block_copy(peer_half, peer_group, "here").wait_recv()
-
-    finish(other, group)
-
-    @pl.loop(1, groups)
-    def _(step):
-        peer_group = lax.rem(group + step, groups)
-        for peer_half in range(halves):
-            finish(peer_half, peer_group)
-
+
+    def serve(joined_group, point):
+        pl.semaphore_wait(ready.at[joined_group], halves)
+        low = tuple(jnp.where(at > mine, at, 0) for at, mine in zip(point, here))
+        high = tuple(at + 1 for at in point)
+
+        def send(peer_group, _):
+            send_ids(peer_group, None)
+            send_block(peer_group, None)
+
+        box(low, high, send)
+
+    descendants(serve)
+    got[me] = block_buf[me]
+    got_ids[me] = id_buf[me]
+
+    def take(semaphore, ref):
+        pltpu.make_async_copy(ref, ref, semaphore).wait()
+
+    blocks = block_buf.at[pl.ds(0, owners - 1)]
+    lists = id_buf.at[pl.ds(0, owners - 1)]
+    take(id_send, lists)
+    take(block_send, blocks)
     acc_copy.wait()
+    keep_acc.wait()
     for index in range(PIECES):
         row_copy(index).wait()
     keep.wait()
-    keep_acc.wait()
+    take(id_recv, lists)
+    take(block_recv, blocks)
 
 
 def thirds(value):
@@ -293,8 +319,7 @@
             dma((5,)),
             dma((PIECES,)), dma((PIECES,)),
             dma, dma,
-            dma((owners,)), dma((owners,)),
-            dma((owners,)), dma((owners,)),
+            dma, dma, dma, dma,
             pltpu.SemaphoreType.REGULAR((groups,)),
         ],
         compiler_params=pltpu.CompilerParams(

time: 21 us -> 18.6 us (0.89)
  Pallas kernels: 20.2 us -> 17.8 us
    pallas_call x1, Pallas kernels: 14.1 us -> 11.6 us  [per_device(): pl.pallas_call(functools.partial(exchange_kernel, halves, groups), out_sh...]
where the time goes in v2:
time: 18.6 us; the launch traced here: 18.4 us
  Pallas kernels  17.8 us (96%)
  between operations  0.64 us (3%)
    pallas_call x1, Pallas kernels, per_device(): pl.pallas_call(functools.partial(exchange_kernel, halves, groups), out_sh...  11.6 us
    pallas_call x1, Pallas kernels, per_device(): pl.pallas_call(update_kernel, out_shape=(jax.ShapeDtypeStruct((2 * rows_h...  6.15 us

profile of v2, /device:TPU:25, one launch (start us, length us, event | category | flops | bytes accessed | tf_op | source)
XLA Modules:
  0.0 18.4 jit_solution(277953613101777738)
XLA Ops:
  0.6 11.6 %exchange.1 = (f32[16392,128]{1,0:T(8,128)S(1)}, f32[2,2,8192]{2,1,0:T(2,128)S(1)}, f32[32,16,128]{2,1,0:T(8,128)S(1)}, s32[32,1,128]{2,1,0:T(1,128)S(1)}) custom-call(f32[2,8192,128]{2,1,0:T(8,128)} %bitcast.8, f32[2,8192]{1,0:T(2,128)} %bitcast.10, f32[32,16,128]{2,1,0:T(8,128)} %bitcast.9, s32[16,32]{1,0:T(8,128)} %bitcast.11, s32[1,32]{1,0:T(1,128)} %counts.1), custom_call_target="tpu_custom_call" | custom-call | tf_op jit(solution)/shard_map/exchange/pallas_call | solution.py:308
  12.2 6.2 %update.1 = (f32[16392,128]{1,0:T(8,128)S(1)}, f32[2,8192,128]{2,1,0:T(8,128)}, f32[2,8192]{1,0:T(2,128)}) custom-call(f32[16392,128]{1,0:T(8,128)S(1)} %get-tuple-element.8.table_in, f32[2,2,8192]{2,1,0:T(2,128)S(1)} %get-tuple-element.9.pair_acc, f32[32,16,128]{2,1,0:T(8,128)S(1)} %get-tuple-element.10.got, ...), custom_call_target="tpu_custom_call", output_to_operand_aliasing={{0}: (0, {})} | custom-call | tf_op jit(solution)/shard_map/update/pallas_call | solution.py:330

commit v3 on v2

--- a/solution.py
+++ b/solution.py
@@ -13,6 +13,7 @@
 LANES = 128
 MESH = pl.DeviceIdType.MESH
 PIECES = 4
+BATCH = 32
 
 
 def axes_of(groups):
@@ -24,8 +25,8 @@
 
 def exchange_kernel(
     halves, groups, weights, accum, grads, ids_t, counts,
-    table, pair_acc, got, got_ids,
-    block_buf, id_in, count_in, id_pad, id_buf,
+    table, state, got, got_ids,
+    pair_acc, block_buf, id_in, count_in, id_pad, id_buf,
     local_sem, row_send, row_recv, acc_send, acc_recv, block_send, block_recv, id_send, id_recv, ready,
 ):
     half = lax.axis_index("half")
@@ -85,8 +86,8 @@
     id_load.wait()
     count_load.wait()
     slot = lax.broadcasted_iota(jnp.int32, ids_t.shape, 0)
-    id_pad[...] = jnp.full(id_pad.shape, -1, jnp.int32)
-    id_pad[0:slots, 0:owners] = jnp.where(slot < count_in[...], id_in[...], -1)
+    spare = 2 * rows_half
+    id_pad[0:slots, 0:owners] = jnp.where(slot < count_in[...], id_in[...], spare)
     turned = id_pad[...].T
     for owner in range(owners):
         id_buf[owner, 0:1, :] = turned[owner:owner + 1, :]
@@ -165,6 +166,12 @@
     take(block_send, blocks)
     acc_copy.wait()
     keep_acc.wait()
+    acc_rows = rows_half // LANES
+    for old in range(2):
+        line = jnp.where(half == 0, pair_acc[old, 0:1, :], pair_acc[old, 1:2, :])
+        for row in range(acc_rows):
+            at = old * acc_rows + row
+            state[at:at + 1, :] = line[:, row * LANES:(row + 1) * LANES]
     for index in range(PIECES):
         row_copy(index).wait()
     keep.wait()
@@ -185,27 +192,19 @@
 
 
 def update_kernel(
-    table_in, pair_acc, got, got_ids, table, new_weights, new_accum,
-    out_acc, state, id_list, picked, delta, in_sem, out_sem, id_sem,
+    table_in, old_state, got, got_ids, table, new_weights, new_accum,
+    out_acc, id_list, delta, acc_sem, out_sem, id_sem,
 ):
-    half = lax.axis_index("half")
     senders, slots, width = got.shape
     count = senders * slots
-    rows_half = pair_acc.shape[2]
+    acc_rows = old_state.shape[0] // 2
+    rows_half = acc_rows * LANES
     piece = rows_half // PIECES
     spare = 2 * rows_half
-    acc_rows = rows_half // LANES
 
     ids_in = pltpu.make_async_copy(got_ids, id_list, id_sem)
     ids_in.start()
     table[spare:spare + 8, :] = jnp.zeros((8, width), jnp.float32)
-
-    is_low = half == 0
-    for old in range(2):
-        line = jnp.where(is_low, pair_acc[old, 0:1, :], pair_acc[old, 1:2, :])
-        for row in range(acc_rows):
-            at = old * acc_rows + row
-            state[at:at + 1, :] = line[:, row * LANES:(row + 1) * LANES]
 
     lane = lax.broadcasted_iota(jnp.int32, (count, LANES), 1)
     sub = lax.broadcasted_iota(jnp.int32, (count, LANES), 0)
@@ -215,65 +214,40 @@
     wide = jnp.broadcast_to(column, (count, LANES))
     line = wide.T[0:1, :]
     grad_parts = thirds(got[...].reshape(count, width))
-    old_state = state[...]
-    state_parts = thirds(old_state)
-    lane_f = lane.astype(jnp.float32)
+    state_parts = thirds(old_state[...])
     block = min(count, 512)
-    gain = jnp.zeros((2 * acc_rows, 3 * LANES), jnp.float32)
-    high_line = jnp.floor(line * (1.0 / LANES))
+    tall = lax.broadcasted_iota(jnp.int32, (block, 2 * acc_rows), 1).astype(jnp.float32)
+    lane_f = lane[:block].astype(jnp.float32)
+    kept = []
     for start in range(0, count, block):
         key = column[start:start + block]
-        same = key == line
-        hot = jnp.where(same, 1.0, 0.0)
+        hot = jnp.where(key == line, 1.0, 0.0)
         total = joined(jnp.dot(hot.astype(jnp.bfloat16), grad_parts,
                                preferred_element_type=jnp.float32), width)
         at_col = lax.broadcasted_iota(jnp.int32, (block, count), 1)
         at_row = lax.broadcasted_iota(jnp.int32, (block, count), 0) + start
-        earlier = jnp.sum(jnp.where(at_col < at_row, hot, 0.0), axis=1, keepdims=True)
+        before = jnp.where(at_col < at_row // BATCH * BATCH, hot, 0.0)
+        beside = jnp.where((at_col < at_row) & (at_col >= at_row // BATCH * BATCH), hot, 0.0)
+        before = jnp.sum(before, axis=1, keepdims=True)
         high = jnp.floor(key * (1.0 / LANES))
         low = key - high * LANES
-        row_hot = jnp.where(lane_f[:block] == high, 1.0, 0.0).astype(jnp.bfloat16) if acc_rows * 2 == LANES else jnp.where(
-            lax.broadcasted_iota(jnp.int32, (block, 2 * acc_rows), 1).astype(jnp.float32) == high, 1.0, 0.0).astype(jnp.bfloat16)
+        row_hot = jnp.where(tall == high, 1.0, 0.0).astype(jnp.bfloat16)
         state_rows = joined(jnp.dot(row_hot, state_parts, preferred_element_type=jnp.float32), LANES)
-        at_low = lane_f[:block] == low
+        at_low = lane_f == low
         old_acc = jnp.sum(jnp.where(at_low, state_rows, 0.0), axis=1, keepdims=True)
         square = jnp.sum(total * total, axis=1, keepdims=True) * (1.0 / width)
-        delta[start:start + block, :] = LEARN_RATE * total / (jnp.sqrt(old_acc + square) + EPSILON)
-        once = jnp.where((earlier == 0.0) & (key >= 0.0), square, 0.0)
-        add_parts = thirds(jnp.where(at_low, once, 0.0))
-        high_of = high_line[:, start:start + block]
-        tall = lax.broadcasted_iota(jnp.int32, (2 * acc_rows, block), 0).astype(jnp.float32)
-        tall_hot = jnp.where(tall == high_of, 1.0, 0.0).astype(jnp.bfloat16)
-        gain = gain + jnp.dot(tall_hot, add_parts, preferred_element_type=jnp.float32)
-    state[...] = old_state + joined(gain, LANES)
-    for old in range(2):
-        for row in range(acc_rows):
-            at = old * acc_rows + row
-            out_acc[old:old + 1, row * LANES:(row + 1) * LANES] = state[at:at + 1, :]
-
-    acc_out = pltpu.make_async_copy(out_acc, new_accum, in_sem)
-    acc_out.start()
+        step = LEARN_RATE * total / (jnp.sqrt(old_acc + square) + EPSILON)
+        delta[start:start + block, :] = jnp.where(before == 0.0, step, 0.0)
+        kept.append((square, before, beside, at_low))
     ids_in.wait()
 
-    def place(sender, slot):
-        at = id_list[sender, 0, slot]
-        return jnp.where(at < 0, spare, at)
-
-    @pl.loop(0, senders)
-    def _(sender):
-        base = pl.multiple_of(sender * slots, slots)
-        rows = [table[pl.ds(place(sender, slot), 1), :] for slot in range(slots)]
-        for slot in range(slots):
-            picked[pl.ds(base + slot, 1), :] = rows[slot]
-
-    picked[...] = picked[...] - delta[...]
-
-    @pl.loop(0, senders)
-    def _(sender):
-        base = pl.multiple_of(sender * slots, slots)
-        rows = [picked[pl.ds(base + slot, 1), :] for slot in range(slots)]
-        for slot in range(slots):
-            table[pl.ds(place(sender, slot), 1), :] = rows[slot]
+    @pl.loop(0, count // BATCH)
+    def _(batch):
+        base = pl.multiple_of(batch * BATCH, BATCH)
+        places = [id_list[batch * (BATCH // slots) + at // slots, 0, at % slots] for at in range(BATCH)]
+        rows = [table[pl.ds(places[at], 1), :] - delta[pl.ds(base + at, 1), :] for at in range(BATCH)]
+        for at in range(BATCH):
+            table[pl.ds(places[at], 1), :] = rows[at]
 
     stores = []
     for old in range(2):
@@ -284,6 +258,24 @@
                 out_sem.at[old * PIECES + index]))
     for store in stores:
         store.start()
+
+    gain = jnp.zeros((2 * acc_rows, 3 * LANES), jnp.float32)
+    high_line = jnp.floor(line * (1.0 / LANES))
+    for index, (square, before, beside, at_low) in enumerate(kept):
+        start = index * block
+        earlier = before + jnp.sum(beside, axis=1, keepdims=True)
+        once = jnp.where(earlier == 0.0, square, 0.0)
+        add_parts = thirds(jnp.where(at_low, once, 0.0))
+        down = lax.broadcasted_iota(jnp.int32, (2 * acc_rows, block), 0).astype(jnp.float32)
+        tall_hot = jnp.where(down == high_line[:, start:start + block], 1.0, 0.0).astype(jnp.bfloat16)
+        gain = gain + jnp.dot(tall_hot, add_parts, preferred_element_type=jnp.float32)
+    new_state = old_state[...] + joined(gain, LANES)
+    for old in range(2):
+        for row in range(acc_rows):
+            at = old * acc_rows + row
+            out_acc[old:old + 1, row * LANES:(row + 1) * LANES] = new_state[at:at + 1, :]
+    acc_out = pltpu.make_async_copy(out_acc, new_accum, acc_sem)
+    acc_out.start()
     for store in stores:
         store.wait()
     acc_out.wait()
@@ -293,7 +285,6 @@
     owners, slots, width = grads.shape[1:]
     rows_half = weights.shape[3]
     table = weights[0, 0]
-    state = accum[0, 0]
     count = owners * slots
     hbm = pl.BlockSpec(memory_space=pltpu.HBM)
     vmem = pl.BlockSpec(memory_space=pltpu.VMEM)
@@ -301,16 +292,17 @@
     dma = pltpu.SemaphoreType.DMA
     landed = (
         jax.ShapeDtypeStruct((2 * rows_half + 8, width), jnp.float32),
-        jax.ShapeDtypeStruct((2, 2, rows_half), jnp.float32),
+        jax.ShapeDtypeStruct((2 * rows_half // LANES, LANES), jnp.float32),
         jax.ShapeDtypeStruct((owners, slots, width), jnp.float32),
         jax.ShapeDtypeStruct((owners, 1, LANES), jnp.int32),
     )
-    moved, pair_acc, got, got_ids = pl.pallas_call(
+    moved, state, got, got_ids = pl.pallas_call(
         functools.partial(exchange_kernel, halves, groups),
         out_shape=landed,
         in_specs=[hbm] * 5,
         out_specs=(vmem,) * 4,
         scratch_shapes=[
+            pltpu.VMEM((2, 2, rows_half), jnp.float32),
             pltpu.VMEM((owners, slots, width), jnp.float32),
             pltpu.VMEM((slots, owners), jnp.int32),
             pltpu.VMEM((1, owners), jnp.int32),
@@ -326,7 +318,7 @@
             collective_id=0, has_side_effects=True, vmem_limit_bytes=16 << 20),
         name="exchange",
     )(*(pltpu.with_memory_space_constraint(value, pltpu.HBM)
-        for value in (table, state, grads[0], row_ids[0].T, counts)))
+        for value in (table, accum[0, 0], grads[0], row_ids[0].T, counts)))
     _, new_weights, new_accum = pl.pallas_call(
         update_kernel,
         out_shape=(
@@ -338,16 +330,14 @@
         out_specs=(vmem, hbm, hbm),
         scratch_shapes=[
             pltpu.VMEM((2, rows_half), jnp.float32),
-            pltpu.VMEM((2 * rows_half // LANES, LANES), jnp.float32),
             pltpu.SMEM((owners, 1, LANES), jnp.int32),
-            pltpu.VMEM((count, width), jnp.float32),
             pltpu.VMEM((count, width), jnp.float32),
             dma, dma((2 * PIECES,)), dma,
         ],
         input_output_aliases={0: 0},
         compiler_params=pltpu.CompilerParams(vmem_limit_bytes=32 << 20),
         name="update",
-    )(moved, pair_acc, got, got_ids)
+    )(moved, state, got, got_ids)
     return new_weights[None, None], new_accum[None, None]
 
 

time: 18.6 us -> 18 us (0.968)
  Pallas kernels: 17.8 us -> 17.1 us
    pallas_call x1, Pallas kernels: 6.15 us -> 5.51 us  [per_device(): pl.pallas_call(update_kernel, out_shape=(jax.ShapeDtypeStruct((2 * rows_h...]
where the time goes in v3:
time: 18 us; the launch traced here: 17.8 us
  Pallas kernels  17.1 us (95%)
  between operations  0.64 us (4%)
    pallas_call x1, Pallas kernels, per_device(): pl.pallas_call(functools.partial(exchange_kernel, halves, groups), out_sh...  11.6 us
    pallas_call x1, Pallas kernels, per_device(): pl.pallas_call(update_kernel, out_shape=(jax.ShapeDtypeStruct((2 * rows_h...  5.51 us

profile of v3, /device:TPU:25, one launch (start us, length us, event | category | flops | bytes accessed | tf_op | source)
XLA Modules:
  0.0 17.8 jit_solution(7863290341512145887)
XLA Ops:
  0.6 11.6 %exchange.1 = (f32[16392,128]{1,0:T(8,128)S(1)}, f32[128,128]{1,0:T(8,128)S(1)}, f32[32,16,128]{2,1,0:T(8,128)S(1)}, s32[32,1,128]{2,1,0:T(1,128)S(1)}) custom-call(f32[2,8192,128]{2,1,0:T(8,128)} %bitcast.8, f32[2,8192]{1,0:T(2,128)} %bitcast.10, f32[32,16,128]{2,1,0:T(8,128)} %bitcast.9, s32[16,32]{1,0:T(8,128)} %bitcast.11, s32[1,32]{1,0:T(1,128)} %counts.1), custom_call_target="tpu_custom_call" | custom-call | tf_op jit(solution)/shard_map/exchange/pallas_call | solution.py:299
  12.2 5.5 %update.1 = (f32[16392,128]{1,0:T(8,128)S(1)}, f32[2,8192,128]{2,1,0:T(8,128)}, f32[2,8192]{1,0:T(2,128)}) custom-call(f32[16392,128]{1,0:T(8,128)S(1)} %get-tuple-element.8.table_in, f32[128,128]{1,0:T(8,128)S(1)} %get-tuple-element.9.old_state, f32[32,16,128]{2,1,0:T(8,128)S(1)} %get-tuple-element.10.got, ...), custom_call_target="tpu_custom_call", output_to_operand_aliasing={{0}: (0, {})} | custom-call | tf_op jit(solution)/shard_map/update/pallas_call | solution.py:322

commit v4 on v3

--- a/solution.py
+++ b/solution.py
@@ -13,7 +13,7 @@
 LANES = 128
 MESH = pl.DeviceIdType.MESH
 PIECES = 4
-BATCH = 32
+GROUP = 16
 
 
 def axes_of(groups):
@@ -83,6 +83,47 @@
             pl.semaphore_signal(barrier, inc=1, device_id=(peer_half, peer_group), device_id_type=MESH)
 
     descendants(greet)
+    pl.semaphore_wait(barrier, halves * past[0] * past[1] * past[2] - 1)
+
+    def announce(peer_group, _):
+        for peer_half in range(halves):
+            pl.semaphore_signal(
+                ready.at[group], inc=1, device_id=(peer_half, peer_group), device_id_type=MESH)
+
+    ancestors(announce)
+
+    def block_copy(peer_half, peer_group):
+        return pltpu.make_async_remote_copy(
+            src_ref=block_buf.at[peer_half * groups + peer_group], dst_ref=got.at[me],
+            send_sem=block_send, recv_sem=block_recv,
+            device_id=(peer_half, peer_group), device_id_type=MESH)
+
+    def id_copy(peer_half, peer_group):
+        return pltpu.make_async_remote_copy(
+            src_ref=id_buf.at[peer_half * groups + peer_group], dst_ref=got_ids.at[me],
+            send_sem=id_send, recv_sem=id_recv,
+            device_id=(peer_half, peer_group), device_id_type=MESH)
+
+    def send(peer_group, _):
+        for peer_half in range(halves):
+            id_copy(peer_half, peer_group).start()
+            block_copy(peer_half, peer_group).start()
+
+    def row_copy(index):
+        rows = pl.ds(index * piece, piece)
+        return pltpu.make_async_remote_copy(
+            src_ref=weights.at[other, rows],
+            dst_ref=table.at[pl.ds(pl.multiple_of(home + index * piece, piece), piece)],
+            send_sem=row_send.at[index], recv_sem=row_recv.at[index],
+            device_id=(other, group), device_id_type=MESH)
+
+    acc_copy = pltpu.make_async_remote_copy(
+        src_ref=accum, dst_ref=pair_acc.at[half], send_sem=acc_send, recv_sem=acc_recv,
+        device_id=(other, group), device_id_type=MESH)
+    acc_copy.start()
+    for index in range(PIECES):
+        row_copy(index).start()
+
     id_load.wait()
     count_load.wait()
     slot = lax.broadcasted_iota(jnp.int32, ids_t.shape, 0)
@@ -92,51 +133,7 @@
     for owner in range(owners):
         id_buf[owner, 0:1, :] = turned[owner:owner + 1, :]
     load.wait()
-    pl.semaphore_wait(barrier, halves * past[0] * past[1] * past[2] - 1)
-
-    def announce(peer_group, _):
-        for peer_half in range(halves):
-            pl.semaphore_signal(
-                ready.at[group], inc=1, device_id=(peer_half, peer_group), device_id_type=MESH)
-
-    ancestors(announce)
-
-    def block_copy(peer_half, peer_group):
-        return pltpu.make_async_remote_copy(
-            src_ref=block_buf.at[peer_half * groups + peer_group], dst_ref=got.at[me],
-            send_sem=block_send, recv_sem=block_recv,
-            device_id=(peer_half, peer_group), device_id_type=MESH)
-
-    def id_copy(peer_half, peer_group):
-        return pltpu.make_async_remote_copy(
-            src_ref=id_buf.at[peer_half * groups + peer_group], dst_ref=got_ids.at[me],
-            send_sem=id_send, recv_sem=id_recv,
-            device_id=(peer_half, peer_group), device_id_type=MESH)
-
-    def send_ids(peer_group, _):
-        for peer_half in range(halves):
-            id_copy(peer_half, peer_group).start()
-
-    def send_block(peer_group, _):
-        for peer_half in range(halves):
-            block_copy(peer_half, peer_group).start()
-
-    def row_copy(index):
-        rows = pl.ds(index * piece, piece)
-        return pltpu.make_async_remote_copy(
-            src_ref=weights.at[other, rows],
-            dst_ref=table.at[pl.ds(pl.multiple_of(home + index * piece, piece), piece)],
-            send_sem=row_send.at[index], recv_sem=row_recv.at[index],
-            device_id=(other, group), device_id_type=MESH)
-
-    acc_copy = pltpu.make_async_remote_copy(
-        src_ref=accum, dst_ref=pair_acc.at[half], send_sem=acc_send, recv_sem=acc_recv,
-        device_id=(other, group), device_id_type=MESH)
-    acc_copy.start()
-    for index in range(PIECES):
-        row_copy(index).start()
-    ancestors(send_ids)
-    ancestors(send_block)
+    ancestors(send)
     id_copy(other, group).start()
     block_copy(other, group).start()
     keep.start()
@@ -146,11 +143,6 @@
         pl.semaphore_wait(ready.at[joined_group], halves)
         low = tuple(jnp.where(at > mine, at, 0) for at, mine in zip(point, here))
         high = tuple(at + 1 for at in point)
-
-        def send(peer_group, _):
-            send_ids(peer_group, None)
-            send_block(peer_group, None)
-
         box(low, high, send)
 
     descendants(serve)
@@ -193,7 +185,7 @@
 
 def update_kernel(
     table_in, old_state, got, got_ids, table, new_weights, new_accum,
-    out_acc, id_list, delta, acc_sem, out_sem, id_sem,
+    out_acc, id_list, picked, column_kept, square_kept, acc_sem, out_sem, id_sem,
 ):
     senders, slots, width = got.shape
     count = senders * slots
@@ -201,6 +193,7 @@
     rows_half = acc_rows * LANES
     piece = rows_half // PIECES
     spare = 2 * rows_half
+    block = min(count, 512)
 
     ids_in = pltpu.make_async_copy(got_ids, id_list, id_sem)
     ids_in.start()
@@ -212,42 +205,58 @@
     mine = jnp.where(lane == lax.rem(sub, slots), spread, 0).astype(jnp.float32)
     column = jnp.sum(mine, axis=1, keepdims=True)
     wide = jnp.broadcast_to(column, (count, LANES))
+    column_kept[...] = wide
     line = wide.T[0:1, :]
     grad_parts = thirds(got[...].reshape(count, width))
     state_parts = thirds(old_state[...])
-    block = min(count, 512)
     tall = lax.broadcasted_iota(jnp.int32, (block, 2 * acc_rows), 1).astype(jnp.float32)
     lane_f = lane[:block].astype(jnp.float32)
-    kept = []
+
+    def each_row(start, act):
+        for at in range(0, block, GROUP):
+            sender = (start + at) // slots
+            act(start + at, [id_list[sender + index // slots, 0, index % slots] for index in range(GROUP)])
+
+    def gather(base, places):
+        rows = [table[pl.ds(place, 1), :] for place in places]
+        for index, row in enumerate(rows):
+            picked[pl.ds(base + index, 1), :] = row
+
+    def scatter(base, places):
+        rows = [picked[pl.ds(base + index, 1), :] for index in range(GROUP)]
+        for place, row in zip(places, rows):
+            table[pl.ds(place, 1), :] = row
+
+    def over_blocks(act):
+        if count == block:
+            each_row(0, act)
+        else:
+            @pl.loop(0, count // block)
+            def _(index):
+                each_row(index * block, act)
+
+    sums = []
     for start in range(0, count, block):
         key = column[start:start + block]
-        hot = jnp.where(key == line, 1.0, 0.0)
-        total = joined(jnp.dot(hot.astype(jnp.bfloat16), grad_parts,
-                               preferred_element_type=jnp.float32), width)
-        at_col = lax.broadcasted_iota(jnp.int32, (block, count), 1)
-        at_row = lax.broadcasted_iota(jnp.int32, (block, count), 0) + start
-        before = jnp.where(at_col < at_row // BATCH * BATCH, hot, 0.0)
-        beside = jnp.where((at_col < at_row) & (at_col >= at_row // BATCH * BATCH), hot, 0.0)
-        before = jnp.sum(before, axis=1, keepdims=True)
+        hot = jnp.where(key == line, 1.0, 0.0).astype(jnp.bfloat16)
+        total = joined(jnp.dot(hot, grad_parts, preferred_element_type=jnp.float32), width)
         high = jnp.floor(key * (1.0 / LANES))
         low = key - high * LANES
         row_hot = jnp.where(tall == high, 1.0, 0.0).astype(jnp.bfloat16)
         state_rows = joined(jnp.dot(row_hot, state_parts, preferred_element_type=jnp.float32), LANES)
-        at_low = lane_f == low
-        old_acc = jnp.sum(jnp.where(at_low, state_rows, 0.0), axis=1, keepdims=True)
+        sums.append((total, jnp.where(lane_f == low, state_rows, 0.0)))
+
+    ids_in.wait()
+    over_blocks(gather)
+    for index, (total, state_rows) in enumerate(sums):
+        start = index * block
+        old_acc = jnp.sum(state_rows, axis=1, keepdims=True)
         square = jnp.sum(total * total, axis=1, keepdims=True) * (1.0 / width)
+        square_kept[start:start + block, :] = jnp.broadcast_to(square, (block, LANES))
         step = LEARN_RATE * total / (jnp.sqrt(old_acc + square) + EPSILON)
-        delta[start:start + block, :] = jnp.where(before == 0.0, step, 0.0)
-        kept.append((square, before, beside, at_low))
-    ids_in.wait()
-
-    @pl.loop(0, count // BATCH)
-    def _(batch):
-        base = pl.multiple_of(batch * BATCH, BATCH)
-        places = [id_list[batch * (BATCH // slots) + at // slots, 0, at % slots] for at in range(BATCH)]
-        rows = [table[pl.ds(places[at], 1), :] - delta[pl.ds(base + at, 1), :] for at in range(BATCH)]
-        for at in range(BATCH):
-            table[pl.ds(places[at], 1), :] = rows[at]
+        picked[start:start + block, :] = picked[start:start + block, :] - step
+
+    over_blocks(scatter)
 
     stores = []
     for old in range(2):
@@ -258,23 +267,32 @@
                 out_sem.at[old * PIECES + index]))
     for store in stores:
         store.start()
-
-    gain = jnp.zeros((2 * acc_rows, 3 * LANES), jnp.float32)
-    high_line = jnp.floor(line * (1.0 / LANES))
-    for index, (square, before, beside, at_low) in enumerate(kept):
-        start = index * block
-        earlier = before + jnp.sum(beside, axis=1, keepdims=True)
-        once = jnp.where(earlier == 0.0, square, 0.0)
-        add_parts = thirds(jnp.where(at_low, once, 0.0))
-        down = lax.broadcasted_iota(jnp.int32, (2 * acc_rows, block), 0).astype(jnp.float32)
-        tall_hot = jnp.where(down == high_line[:, start:start + block], 1.0, 0.0).astype(jnp.bfloat16)
-        gain = gain + jnp.dot(tall_hot, add_parts, preferred_element_type=jnp.float32)
-    new_state = old_state[...] + joined(gain, LANES)
-    for old in range(2):
-        for row in range(acc_rows):
-            at = old * acc_rows + row
-            out_acc[old:old + 1, row * LANES:(row + 1) * LANES] = new_state[at:at + 1, :]
     acc_out = pltpu.make_async_copy(out_acc, new_accum, acc_sem)
+
+    @pl.when(lax.axis_index("half") >= 0)
+    def _():
+        keys = column_kept[...]
+        across = keys.T[0:1, :]
+        high_line = jnp.floor(across * (1.0 / LANES))
+        gain = jnp.zeros((2 * acc_rows, 3 * LANES), jnp.float32)
+        for start in range(0, count, block):
+            key = keys[start:start + block, 0:1]
+            at_col = lax.broadcasted_iota(jnp.int32, (block, count), 1)
+            at_row = lax.broadcasted_iota(jnp.int32, (block, count), 0) + start
+            earlier = jnp.sum(
+                jnp.where((at_col < at_row) & (key == across), 1.0, 0.0), axis=1, keepdims=True)
+            low = keys[start:start + block] - jnp.floor(keys[start:start + block] * (1.0 / LANES)) * LANES
+            once = jnp.where((lane_f == low) & (earlier == 0.0), square_kept[start:start + block, :], 0.0)
+            add_parts = thirds(once)
+            down = lax.broadcasted_iota(jnp.int32, (2 * acc_rows, block), 0).astype(jnp.float32)
+            tall_hot = jnp.where(down == high_line[:, start:start + block], 1.0, 0.0).astype(jnp.bfloat16)
+            gain = gain + jnp.dot(tall_hot, add_parts, preferred_element_type=jnp.float32)
+        new_state = old_state[...] + joined(gain, LANES)
+        for old in range(2):
+            for row in range(acc_rows):
+                at = old * acc_rows + row
+                out_acc[old:old + 1, row * LANES:(row + 1) * LANES] = new_state[at:at + 1, :]
+
     acc_out.start()
     for store in stores:
         store.wait()
@@ -332,6 +350,8 @@
             pltpu.VMEM((2, rows_half), jnp.float32),
             pltpu.SMEM((owners, 1, LANES), jnp.int32),
             pltpu.VMEM((count, width), jnp.float32),
+            pltpu.VMEM((count, LANES), jnp.float32),
+            pltpu.VMEM((count, LANES), jnp.float32),
             dma, dma((2 * PIECES,)), dma,
         ],
         input_output_aliases={0: 0},

time: 18 us -> 16.8 us (0.933)
  Pallas kernels: 17.1 us -> 15.9 us
    pallas_call x1, Pallas kernels: 5.51 us -> 4.76 us  [per_device(): pl.pallas_call(update_kernel, out_shape=(jax.ShapeDtypeStruct((2 * rows_h...]
    pallas_call x1, Pallas kernels: 11.6 us -> 11.2 us  [per_device(): pl.pallas_call(functools.partial(exchange_kernel, halves, groups), out_sh...]
where the time goes in v4:
time: 16.8 us; the launch traced here: 16.6 us
  Pallas kernels  15.9 us (95%)
  between operations  0.64 us (4%)
    pallas_call x1, Pallas kernels, per_device(): pl.pallas_call(functools.partial(exchange_kernel, halves, groups), out_sh...  11.2 us
    pallas_call x1, Pallas kernels, per_device(): pl.pallas_call(update_kernel, out_shape=(jax.ShapeDtypeStruct((2 * rows_h...  4.76 us

profile of v4, /device:TPU:25, one launch (start us, length us, event | category | flops | bytes accessed | tf_op | source)
XLA Modules:
  0.0 16.6 jit_solution(3891471948762154610)
XLA Ops:
  0.6 11.2 %exchange.1 = (f32[16392,128]{1,0:T(8,128)S(1)}, f32[128,128]{1,0:T(8,128)S(1)}, f32[32,16,128]{2,1,0:T(8,128)S(1)}, s32[32,1,128]{2,1,0:T(1,128)S(1)}) custom-call(f32[2,8192,128]{2,1,0:T(8,128)} %bitcast.8, f32[2,8192]{1,0:T(2,128)} %bitcast.10, f32[32,16,128]{2,1,0:T(8,128)} %bitcast.9, s32[16,32]{1,0:T(8,128)} %bitcast.11, s32[1,32]{1,0:T(1,128)} %counts.1), custom_call_target="tpu_custom_call" | custom-call | tf_op jit(solution)/shard_map/exchange/pallas_call | solution.py:317
  11.8 4.8 %update.1 = (f32[16392,128]{1,0:T(8,128)S(1)}, f32[2,8192,128]{2,1,0:T(8,128)}, f32[2,8192]{1,0:T(2,128)}) custom-call(f32[16392,128]{1,0:T(8,128)S(1)} %get-tuple-element.8.table_in, f32[128,128]{1,0:T(8,128)S(1)} %get-tuple-element.9.old_state, f32[32,16,128]{2,1,0:T(8,128)S(1)} %get-tuple-element.10.got, ...), custom_call_target="tpu_custom_call", output_to_operand_aliasing={{0}: (0, {})} | custom-call | tf_op jit(solution)/shard_map/update/pallas_call | solution.py:340

commit v5 on v4

--- a/solution.py
+++ b/solution.py
@@ -105,9 +105,10 @@
             device_id=(peer_half, peer_group), device_id_type=MESH)
 
     def send(peer_group, _):
-        for peer_half in range(halves):
+        for turn in range(halves):
+            peer_half = lax.rem(half + turn + 1, halves)
+            block_copy(peer_half, peer_group).start()
             id_copy(peer_half, peer_group).start()
-            block_copy(peer_half, peer_group).start()
 
     def row_copy(index):
         rows = pl.ds(index * piece, piece)
@@ -133,7 +134,20 @@
     for owner in range(owners):
         id_buf[owner, 0:1, :] = turned[owner:owner + 1, :]
     load.wait()
-    ancestors(send)
+    def wave(act):
+        @pl.loop(0, at_a + at_b + at_c)
+        def _(distance):
+            @pl.loop(0, past[1])
+            def _(b):
+                @pl.loop(0, past[2])
+                def _(c):
+                    a = distance - b - c
+
+                    @pl.when((a >= 0) & (a <= at_a))
+                    def _():
+                        act((a * size_b + b) * size_c + c, (a, b, c))
+
+    wave(send)
     id_copy(other, group).start()
     block_copy(other, group).start()
     keep.start()
@@ -145,7 +159,18 @@
         high = tuple(at + 1 for at in point)
         box(low, high, send)
 
-    descendants(serve)
+    @pl.loop(1, size_a + size_b + size_c - at_a - at_b - at_c - 2)
+    def _(distance):
+        @pl.loop(at_b, size_b)
+        def _(b):
+            @pl.loop(at_c, size_c)
+            def _(c):
+                a = at_a + distance - (b - at_b) - (c - at_c)
+
+                @pl.when((a >= at_a) & (a < size_a))
+                def _():
+                    serve((a * size_b + b) * size_c + c, (a, b, c))
+
     got[me] = block_buf[me]
     got_ids[me] = id_buf[me]
 
@@ -195,8 +220,12 @@
     spare = 2 * rows_half
     block = min(count, 512)
 
-    ids_in = pltpu.make_async_copy(got_ids, id_list, id_sem)
-    ids_in.start()
+    part = senders // 2
+    ids_in = [
+        pltpu.make_async_copy(got_ids.at[pl.ds(at, part)], id_list.at[pl.ds(at, part)], id_sem.at[at // part])
+        for at in (0, part)]
+    for copy in ids_in:
+        copy.start()
     table[spare:spare + 8, :] = jnp.zeros((8, width), jnp.float32)
 
     lane = lax.broadcasted_iota(jnp.int32, (count, LANES), 1)
@@ -212,8 +241,8 @@
     tall = lax.broadcasted_iota(jnp.int32, (block, 2 * acc_rows), 1).astype(jnp.float32)
     lane_f = lane[:block].astype(jnp.float32)
 
-    def each_row(start, act):
-        for at in range(0, block, GROUP):
+    def each_row(start, length, act):
+        for at in range(0, length, GROUP):
             sender = (start + at) // slots
             act(start + at, [id_list[sender + index // slots, 0, index % slots] for index in range(GROUP)])
 
@@ -229,11 +258,11 @@
 
     def over_blocks(act):
         if count == block:
-            each_row(0, act)
+            each_row(0, block, act)
         else:
             @pl.loop(0, count // block)
             def _(index):
-                each_row(index * block, act)
+                each_row(index * block, block, act)
 
     sums = []
     for start in range(0, count, block):
@@ -246,8 +275,15 @@
         state_rows = joined(jnp.dot(row_hot, state_parts, preferred_element_type=jnp.float32), LANES)
         sums.append((total, jnp.where(lane_f == low, state_rows, 0.0)))
 
-    ids_in.wait()
-    over_blocks(gather)
+    if count == block:
+        ids_in[0].wait()
+        each_row(0, block // 2, gather)
+        ids_in[1].wait()
+        each_row(block // 2, block // 2, gather)
+    else:
+        for copy in ids_in:
+            copy.wait()
+        over_blocks(gather)
     for index, (total, state_rows) in enumerate(sums):
         start = index * block
         old_acc = jnp.sum(state_rows, axis=1, keepdims=True)
@@ -352,7 +388,7 @@
             pltpu.VMEM((count, width), jnp.float32),
             pltpu.VMEM((count, LANES), jnp.float32),
             pltpu.VMEM((count, LANES), jnp.float32),
-            dma, dma((2 * PIECES,)), dma,
+            dma, dma((2 * PIECES,)), dma((2,)),
         ],
         input_output_aliases={0: 0},
         compiler_params=pltpu.CompilerParams(vmem_limit_bytes=32 << 20),

time: 16.8 us -> 16.7 us (level)
  the two profiles are of different devices: /device:TPU:25 before, /device:TPU:24 now
where the time goes in v5:
time: 16.7 us; the launch traced here: 16.5 us
  Pallas kernels  15.9 us (95%)
  between operations  0.64 us (4%)
    pallas_call x1, Pallas kernels, per_device(): pl.pallas_call(functools.partial(exchange_kernel, halves, groups), out_sh...  11.2 us
    pallas_call x1, Pallas kernels, per_device(): pl.pallas_call(update_kernel, out_shape=(jax.ShapeDtypeStruct((2 * rows_h...  4.72 us

profile of v5, /device:TPU:24, one launch (start us, length us, event | category | flops | bytes accessed | tf_op | source)
XLA Modules:
  0.0 16.5 jit_solution(15772529769726686035)
XLA Ops:
  0.6 11.2 %exchange.1 = (f32[16392,128]{1,0:T(8,128)S(1)}, f32[128,128]{1,0:T(8,128)S(1)}, f32[32,16,128]{2,1,0:T(8,128)S(1)}, s32[32,1,128]{2,1,0:T(1,128)S(1)}) custom-call(f32[2,8192,128]{2,1,0:T(8,128)} %bitcast.8, f32[2,8192]{1,0:T(2,128)} %bitcast.10, f32[32,16,128]{2,1,0:T(8,128)} %bitcast.9, s32[16,32]{1,0:T(8,128)} %bitcast.11, s32[1,32]{1,0:T(1,128)} %counts.1), custom_call_target="tpu_custom_call" | custom-call | tf_op jit(solution)/shard_map/exchange/pallas_call | solution.py:353
  11.8 4.7 %update.1 = (f32[16392,128]{1,0:T(8,128)S(1)}, f32[2,8192,128]{2,1,0:T(8,128)}, f32[2,8192]{1,0:T(2,128)}) custom-call(f32[16392,128]{1,0:T(8,128)S(1)} %get-tuple-element.8.table_in, f32[128,128]{1,0:T(8,128)S(1)} %get-tuple-element.9.old_state, f32[32,16,128]{2,1,0:T(8,128)S(1)} %get-tuple-element.10.got, ...), custom_call_target="tpu_custom_call", output_to_operand_aliasing={{0}: (0, {})} | custom-call | tf_op jit(solution)/shard_map/update/pallas_call | solution.py:376

commit v6 on v5

--- a/solution.py
+++ b/solution.py
@@ -25,8 +25,8 @@
 
 def exchange_kernel(
     halves, groups, weights, accum, grads, ids_t, counts,
-    table, state, got, got_ids,
-    pair_acc, block_buf, id_in, count_in, id_pad, id_buf,
+    table, state, got, column_kept, lines,
+    got_ids, pair_acc, block_buf, id_in, count_in, id_pad, id_buf,
     local_sem, row_send, row_recv, acc_send, acc_recv, block_send, block_recv, id_send, id_recv, ready,
 ):
     half = lax.axis_index("half")
@@ -104,11 +104,13 @@
             send_sem=id_send, recv_sem=id_recv,
             device_id=(peer_half, peer_group), device_id_type=MESH)
 
-    def send(peer_group, _):
+    def send_ids(peer_group, _):
         for turn in range(halves):
-            peer_half = lax.rem(half + turn + 1, halves)
-            block_copy(peer_half, peer_group).start()
-            id_copy(peer_half, peer_group).start()
+            id_copy(lax.rem(half + turn + 1, halves), peer_group).start()
+
+    def send_block(peer_group, _):
+        for turn in range(halves):
+            block_copy(lax.rem(half + turn + 1, halves), peer_group).start()
 
     def row_copy(index):
         rows = pl.ds(index * piece, piece)
@@ -147,7 +149,8 @@
                     def _():
                         act((a * size_b + b) * size_c + c, (a, b, c))
 
-    wave(send)
+    wave(send_ids)
+    wave(send_block)
     id_copy(other, group).start()
     block_copy(other, group).start()
     keep.start()
@@ -157,7 +160,8 @@
         pl.semaphore_wait(ready.at[joined_group], halves)
         low = tuple(jnp.where(at > mine, at, 0) for at, mine in zip(point, here))
         high = tuple(at + 1 for at in point)
-        box(low, high, send)
+        box(low, high, send_ids)
+        box(low, high, send_block)
 
     @pl.loop(1, size_a + size_b + size_c - at_a - at_b - at_c - 2)
     def _(distance):
@@ -179,8 +183,6 @@
 
     blocks = block_buf.at[pl.ds(0, owners - 1)]
     lists = id_buf.at[pl.ds(0, owners - 1)]
-    take(id_send, lists)
-    take(block_send, blocks)
     acc_copy.wait()
     keep_acc.wait()
     acc_rows = rows_half // LANES
@@ -189,11 +191,23 @@
         for row in range(acc_rows):
             at = old * acc_rows + row
             state[at:at + 1, :] = line[:, row * LANES:(row + 1) * LANES]
+    take(id_recv, lists)
+    count = owners * slots
+    lane = lax.broadcasted_iota(jnp.int32, (count, LANES), 1)
+    sub = lax.broadcasted_iota(jnp.int32, (count, LANES), 0)
+    spread = jnp.broadcast_to(got_ids[...], (owners, slots, LANES)).reshape(count, LANES)
+    mine = jnp.where(lane == lax.rem(sub, slots), spread, 0).astype(jnp.float32)
+    wide = jnp.broadcast_to(jnp.sum(mine, axis=1, keepdims=True), (count, LANES))
+    column_kept[...] = wide
+    line = wide.T[0:1, :].astype(jnp.int32)
+    for row in range(count // LANES):
+        lines[row:row + 1, :] = line[:, row * LANES:(row + 1) * LANES]
     for index in range(PIECES):
         row_copy(index).wait()
     keep.wait()
-    take(id_recv, lists)
+    take(id_send, lists)
     take(block_recv, blocks)
+    take(block_send, blocks)
 
 
 def thirds(value):
@@ -209,8 +223,8 @@
 
 
 def update_kernel(
-    table_in, old_state, got, got_ids, table, new_weights, new_accum,
-    out_acc, id_list, picked, column_kept, square_kept, acc_sem, out_sem, id_sem,
+    table_in, old_state, got, column_kept, lines, table, new_weights, new_accum,
+    out_acc, id_list, picked, square_kept, acc_sem, out_sem, id_sem,
 ):
     senders, slots, width = got.shape
     count = senders * slots
@@ -220,31 +234,20 @@
     spare = 2 * rows_half
     block = min(count, 512)
 
-    part = senders // 2
-    ids_in = [
-        pltpu.make_async_copy(got_ids.at[pl.ds(at, part)], id_list.at[pl.ds(at, part)], id_sem.at[at // part])
-        for at in (0, part)]
-    for copy in ids_in:
-        copy.start()
+    ids_in = pltpu.make_async_copy(lines, id_list, id_sem)
+    ids_in.start()
     table[spare:spare + 8, :] = jnp.zeros((8, width), jnp.float32)
 
-    lane = lax.broadcasted_iota(jnp.int32, (count, LANES), 1)
-    sub = lax.broadcasted_iota(jnp.int32, (count, LANES), 0)
-    spread = jnp.broadcast_to(got_ids[...], (senders, slots, LANES)).reshape(count, LANES)
-    mine = jnp.where(lane == lax.rem(sub, slots), spread, 0).astype(jnp.float32)
-    column = jnp.sum(mine, axis=1, keepdims=True)
-    wide = jnp.broadcast_to(column, (count, LANES))
-    column_kept[...] = wide
-    line = wide.T[0:1, :]
+    lane = lax.broadcasted_iota(jnp.int32, (block, LANES), 1)
+    line = jnp.concatenate([lines[row:row + 1, :] for row in range(count // LANES)], axis=1).astype(jnp.float32)
     grad_parts = thirds(got[...].reshape(count, width))
     state_parts = thirds(old_state[...])
     tall = lax.broadcasted_iota(jnp.int32, (block, 2 * acc_rows), 1).astype(jnp.float32)
-    lane_f = lane[:block].astype(jnp.float32)
+    lane_f = lane.astype(jnp.float32)
 
     def each_row(start, length, act):
         for at in range(0, length, GROUP):
-            sender = (start + at) // slots
-            act(start + at, [id_list[sender + index // slots, 0, index % slots] for index in range(GROUP)])
+            act(start + at, [id_list[start // LANES + (at + index) // LANES, (at + index) % LANES] for index in range(GROUP)])
 
     def gather(base, places):
         rows = [table[pl.ds(place, 1), :] for place in places]
@@ -266,7 +269,7 @@
 
     sums = []
     for start in range(0, count, block):
-        key = column[start:start + block]
+        key = column_kept[start:start + block, 0:1]
         hot = jnp.where(key == line, 1.0, 0.0).astype(jnp.bfloat16)
         total = joined(jnp.dot(hot, grad_parts, preferred_element_type=jnp.float32), width)
         high = jnp.floor(key * (1.0 / LANES))
@@ -275,15 +278,8 @@
         state_rows = joined(jnp.dot(row_hot, state_parts, preferred_element_type=jnp.float32), LANES)
         sums.append((total, jnp.where(lane_f == low, state_rows, 0.0)))
 
-    if count == block:
-        ids_in[0].wait()
-        each_row(0, block // 2, gather)
-        ids_in[1].wait()
-        each_row(block // 2, block // 2, gather)
-    else:
-        for copy in ids_in:
-            copy.wait()
-        over_blocks(gather)
+    ids_in.wait()
+    over_blocks(gather)
     for index, (total, state_rows) in enumerate(sums):
         start = index * block
         old_acc = jnp.sum(state_rows, axis=1, keepdims=True)
@@ -348,14 +344,16 @@
         jax.ShapeDtypeStruct((2 * rows_half + 8, width), jnp.float32),
         jax.ShapeDtypeStruct((2 * rows_half // LANES, LANES), jnp.float32),
         jax.ShapeDtypeStruct((owners, slots, width), jnp.float32),
-        jax.ShapeDtypeStruct((owners, 1, LANES), jnp.int32),
+        jax.ShapeDtypeStruct((count, LANES), jnp.float32),
+        jax.ShapeDtypeStruct((count // LANES, LANES), jnp.int32),
     )
-    moved, state, got, got_ids = pl.pallas_call(
+    moved, state, got, column, lines = pl.pallas_call(
         functools.partial(exchange_kernel, halves, groups),
         out_shape=landed,
         in_specs=[hbm] * 5,
-        out_specs=(vmem,) * 4,
+        out_specs=(vmem,) * 5,
         scratch_shapes=[
+            pltpu.VMEM((owners, 1, LANES), jnp.int32),
             pltpu.VMEM((2, 2, rows_half), jnp.float32),
             pltpu.VMEM((owners, slots, width), jnp.float32),
             pltpu.VMEM((slots, owners), jnp.int32),
@@ -380,20 +378,19 @@
             jax.ShapeDtypeStruct((2, rows_half, width), jnp.float32),
             jax.ShapeDtypeStruct((2, rows_half), jnp.float32),
         ),
-        in_specs=[vmem] * 4,
+        in_specs=[vmem] * 5,
         out_specs=(vmem, hbm, hbm),
         scratch_shapes=[
             pltpu.VMEM((2, rows_half), jnp.float32),
-            pltpu.SMEM((owners, 1, LANES), jnp.int32),
+            pltpu.SMEM((count // LANES, LANES), jnp.int32),
             pltpu.VMEM((count, width), jnp.float32),
             pltpu.VMEM((count, LANES), jnp.float32),
-            pltpu.VMEM((count, LANES), jnp.float32),
-            dma, dma((2 * PIECES,)), dma((2,)),
+            dma, dma((2 * PIECES,)), dma,
         ],
         input_output_aliases={0: 0},
         compiler_params=pltpu.CompilerParams(vmem_limit_bytes=32 << 20),
         name="update",
-    )(moved, state, got, got_ids)
+    )(moved, state, got, column, lines)
     return new_weights[None, None], new_accum[None, None]
 
 

time: 16.7 us -> 16.5 us (0.988)
  the two profiles are of different devices: /device:TPU:24 before, /device:TPU:25 now
where the time goes in v6:
time: 16.5 us; the launch traced here: 16.2 us
  Pallas kernels  15.6 us (95%)
  between operations  0.64 us (4%)
    pallas_call x1, Pallas kernels, per_device(): pl.pallas_call(functools.partial(exchange_kernel, halves, groups), out_sh...  11 us
    pallas_call x1, Pallas kernels, per_device(): pl.pallas_call(update_kernel, out_shape=(jax.ShapeDtypeStruct((2 * rows_h...  4.57 us

profile of v6, /device:TPU:25, one launch (start us, length us, event | category | flops | bytes accessed | tf_op | source)
XLA Modules:
  0.0 16.2 jit_solution(11344205406203895953)
XLA Ops:
  0.6 11.0 %exchange.1 = (f32[16392,128]{1,0:T(8,128)S(1)}, f32[128,128]{1,0:T(8,128)S(1)}, f32[32,16,128]{2,1,0:T(8,128)S(1)}, f32[512,128]{1,0:T(8,128)S(1)}, s32[4,128]{1,0:T(4,128)S(1)}) custom-call(f32[2,8192,128]{2,1,0:T(8,128)} %bitcast.8, f32[2,8192]{1,0:T(2,128)} %bitcast.10, f32[32,16,128]{2,1,0:T(8,128)} %bitcast.9, s32[16,32]{1,0:T(8,128)} %bitcast.11, ...), custom_call_target="tpu_custom_call" | custom-call | tf_op jit(solution)/shard_map/exchange/pallas_call | solution.py:350
  11.6 4.6 %update.1 = (f32[16392,128]{1,0:T(8,128)S(1)}, f32[2,8192,128]{2,1,0:T(8,128)}, f32[2,8192]{1,0:T(2,128)}) custom-call(f32[16392,128]{1,0:T(8,128)S(1)} %get-tuple-element.9.table_in, f32[128,128]{1,0:T(8,128)S(1)} %get-tuple-element.10.old_state, f32[32,16,128]{2,1,0:T(8,128)S(1)} %get-tuple-element.11.got, ...), custom_call_target="tpu_custom_call", output_to_operand_aliasing={{0}: (0, {})} | custom-call | tf_op jit(solution)/shard_map/update/pallas_call | solution.py:374

commit v7 on v6

--- a/solution.py
+++ b/solution.py
@@ -13,7 +13,8 @@
 LANES = 128
 MESH = pl.DeviceIdType.MESH
 PIECES = 4
-GROUP = 16
+WRITES = 2
+GROUP = 8
 
 
 def axes_of(groups):
@@ -230,7 +231,7 @@
     count = senders * slots
     acc_rows = old_state.shape[0] // 2
     rows_half = acc_rows * LANES
-    piece = rows_half // PIECES
+    piece = rows_half // WRITES
     spare = 2 * rows_half
     block = min(count, 512)
 
@@ -292,11 +293,11 @@
 
     stores = []
     for old in range(2):
-        for index in range(PIECES):
+        for index in range(WRITES):
             stores.append(pltpu.make_async_copy(
                 table.at[pl.ds(old * rows_half + index * piece, piece)],
                 new_weights.at[old, pl.ds(index * piece, piece)],
-                out_sem.at[old * PIECES + index]))
+                out_sem.at[old * WRITES + index]))
     for store in stores:
         store.start()
     acc_out = pltpu.make_async_copy(out_acc, new_accum, acc_sem)
@@ -385,7 +386,7 @@
             pltpu.SMEM((count // LANES, LANES), jnp.int32),
             pltpu.VMEM((count, width), jnp.float32),
             pltpu.VMEM((count, LANES), jnp.float32),
-            dma, dma((2 * PIECES,)), dma,
+            dma, dma((2 * WRITES,)), dma,
         ],
         input_output_aliases={0: 0},
         compiler_params=pltpu.CompilerParams(vmem_limit_bytes=32 << 20),

time: 16.5 us -> 16.5 us (level)
  no operation moved by 1% of the time
where the time goes in v7:
time: 16.5 us; the launch traced here: 16.2 us
  Pallas kernels  15.6 us (95%)
  between operations  0.64 us (4%)
    pallas_call x1, Pallas kernels, per_device(): pl.pallas_call(functools.partial(exchange_kernel, halves, groups), out_sh...  11 us
    pallas_call x1, Pallas kernels, per_device(): pl.pallas_call(update_kernel, out_shape=(jax.ShapeDtypeStruct((2 * rows_h...  4.56 us

profile of v7, /device:TPU:25, one launch (start us, length us, event | category | flops | bytes accessed | tf_op | source)
XLA Modules:
  0.0 16.2 jit_solution(5293671930626315500)
XLA Ops:
  0.6 11.0 %exchange.1 = (f32[16392,128]{1,0:T(8,128)S(1)}, f32[128,128]{1,0:T(8,128)S(1)}, f32[32,16,128]{2,1,0:T(8,128)S(1)}, f32[512,128]{1,0:T(8,128)S(1)}, s32[4,128]{1,0:T(4,128)S(1)}) custom-call(f32[2,8192,128]{2,1,0:T(8,128)} %bitcast.8, f32[2,8192]{1,0:T(2,128)} %bitcast.10, f32[32,16,128]{2,1,0:T(8,128)} %bitcast.9, s32[16,32]{1,0:T(8,128)} %bitcast.11, ...), custom_call_target="tpu_custom_call" | custom-call | tf_op jit(solution)/shard_map/exchange/pallas_call | solution.py:351
  11.6 4.6 %update.1 = (f32[16392,128]{1,0:T(8,128)S(1)}, f32[2,8192,128]{2,1,0:T(8,128)}, f32[2,8192]{1,0:T(2,128)}) custom-call(f32[16392,128]{1,0:T(8,128)S(1)} %get-tuple-element.9.table_in, f32[128,128]{1,0:T(8,128)S(1)} %get-tuple-element.10.old_state, f32[32,16,128]{2,1,0:T(8,128)S(1)} %get-tuple-element.11.got, ...), custom_call_target="tpu_custom_call", output_to_operand_aliasing={{0}: (0, {})} | custom-call | tf_op jit(solution)/shard_map/update/pallas_call | solution.py:375
